TPU v7x, 32 devices: a whole 2x2x4 slice. The times are simulated.
32 devices in a mesh: strip: 8 (over z, x), seq: 4 (over y, core).
Axes of the slice: x: 2, y: 2, z: 4, core: 2. Of those that a mesh axis runs over, the one named last changes fastest.
Arguments:
- patches: bfloat16 [32, 536, 768], P('strip', 'seq'), may hold values from -6 to 6
- lengths: int32 [32], P('strip'), may hold values from 1 to 536, as said below
- script: int32 [32], P('strip'), may hold values from 0 to 3, as said below
- script_table: bfloat16 [4, 768], replicated, may hold values from -3 to 3
- gain_one: float32 [768], replicated, may hold values from 0.25 to 1.75
- bias_one: float32 [768], replicated, may hold values from -2 to 2
- qkv_weight: bfloat16 [768, 2304], replicated, may hold values from -0.3125 to 0.3125
- query_bias: float32 [768], replicated, may hold values from -3 to 3
- value_bias: float32 [768], replicated, may hold values from -3 to 3
- out_weight: bfloat16 [768, 768], replicated, may hold values from -0.875 to 0.875
- out_bias: float32 [768], replicated, may hold values from -3 to 3
- gain_two: float32 [768], replicated, may hold values from 0.25 to 1.75
- bias_two: float32 [768], replicated, may hold values from -2 to 2
- up_weight: bfloat16 [768, 3072], replicated, may hold values from -0.21875 to 0.21875
- up_bias: float32 [3072], replicated, may hold values from -3 to 3
- down_weight: bfloat16 [3072, 768], replicated, may hold values from -0.109375 to 0.109375
- down_bias: float32 [768], replicated, may hold values from -3 to 3
- cotangent: bfloat16 [32, 536, 768], P('strip', 'seq'), may hold values from -6 to 6
Outputs:
- layer_out: bfloat16 [32, 536, 768], P('strip', 'seq')
- grad_patches: bfloat16 [32, 536, 768], P('strip', 'seq')
- grad_table: float32 [768, 4], P(('strip', 'seq'))
- grad_gain_one: float32 [768], P(('strip', 'seq'))
- grad_bias_one: float32 [768], P(('strip', 'seq'))
- grad_qkv: float32 [768, 2304], P(('strip', 'seq'))
- grad_query_bias: float32 [768], P(('strip', 'seq'))
- grad_value_bias: float32 [768], P(('strip', 'seq'))
- grad_out_weight: float32 [768, 768], P(('strip', 'seq'))
- grad_out_bias: float32 [768], P(('strip', 'seq'))
- grad_gain_two: float32 [768], P(('strip', 'seq'))
- grad_bias_two: float32 [768], P(('strip', 'seq'))
- grad_up_weight: float32 [768, 3072], P(('strip', 'seq'))
- grad_up_bias: float32 [3072], P(('strip', 'seq'))
- grad_down_weight: float32 [3072, 768], P(('strip', 'seq'))
- grad_down_bias: float32 [768], P(('strip', 'seq'))
Inputs may be any that keep to these rules, and one draw needn't show every extreme that they name: The first lengths[s] patch slots of strip s are filled; some strip has all 536 filled. `script`: script ids never fall from one strip to the next.
All inputs are finite; a program needn't handle non-finite values.
Results may differ from a plain program's by a relative error of at most 0.013.
The roundings to bfloat16 on the way count: a program that leaves them out, or rounds other values in their place, can miss the bound.
Values may be sent and summed in bfloat16 or wider, within the bound.
A program may use at most 192 MiB of HBM per device.

v0:
```python
import jax
import jax.numpy as jnp
from jax import lax
from jax.sharding import PartitionSpec as P

HD = 64
epsilon = 1e-12


def normalize(hidden):
    centred = hidden - jnp.mean(hidden, axis=-1, keepdims=True)
    inverse = lax.rsqrt(jnp.mean(centred * centred, axis=-1, keepdims=True) + epsilon)
    return (centred * inverse, inverse)


def norm_back(upstream, gain, normed, inverse):
    scaled = upstream * gain
    return inverse * (
        scaled
        - jnp.mean(scaled, axis=-1, keepdims=True)
        - normed * jnp.mean(scaled * normed, axis=-1, keepdims=True)
    )


def weight_grad(inputs, upstream):
    return lax.dot_general(
        inputs, upstream, (((0,), (0,)), ((), ())), preferred_element_type=jnp.float32
    )


def input_grad(upstream, weight):
    return lax.dot_general(
        upstream, weight, (((1,), (1,)), ((), ())), preferred_element_type=jnp.float32
    )


def gelu_slope(upper):
    return (
        0.5 * (1.0 + lax.erf(upper * 0.7071067811865476))
        + upper * jnp.exp(-0.5 * upper * upper) * 0.3989422804014327
    )


def split_block(block):
    seq_len = block.shape[0]
    heads_here = block.shape[2] // HD
    return [block[:, member].reshape(seq_len, heads_here, HD) for member in range(3)]


def masked_logits(queries, key_rows, length):
    logits = jnp.einsum(
        "qhd,khd->hqk", queries, key_rows, preferred_element_type=jnp.float32
    ) * HD ** (-0.5)
    visible = jnp.arange(logits.shape[-1], dtype=jnp.int32) < length
    return jnp.where(visible[None, None, :], logits, -1000000000.0)


def attend_forward(item):
    block, length = item
    queries, key_rows, values = split_block(block)
    logits = masked_logits(queries, key_rows, length)
    highest = jnp.max(logits, axis=-1, keepdims=True)
    expanded = jnp.exp(logits - highest)
    totals = jnp.sum(expanded, axis=-1, keepdims=True)
    probs = (expanded / totals).astype(jnp.bfloat16)
    mixed = jnp.einsum("hqk,khd->qhd", probs, values, preferred_element_type=jnp.float32)
    mixed = mixed.astype(jnp.bfloat16).reshape(block.shape[0], block.shape[2])
    return (mixed, (highest + jnp.log(totals))[..., 0])


def attend_backward(item):
    block, log_total, grad_mixed, length = item
    queries, key_rows, values = split_block(block)
    logits = masked_logits(queries, key_rows, length)
    probs = jnp.exp(logits - log_total[..., None])
    grad_heads = grad_mixed.reshape(queries.shape)
    grad_values = jnp.einsum(
        "hqk,qhd->khd", probs.astype(jnp.bfloat16), grad_heads, preferred_element_type=jnp.float32
    )
    grad_probs = jnp.einsum("qhd,khd->hqk", grad_heads, values, preferred_element_type=jnp.float32)
    inner = jnp.sum(probs * grad_probs, axis=-1, keepdims=True)
    grad_logits = (probs * (grad_probs - inner)).astype(jnp.bfloat16)
    grad_queries = jnp.einsum(
        "hqk,khd->qhd", grad_logits, key_rows, preferred_element_type=jnp.float32
    ) * HD ** (-0.5)
    grad_keys = jnp.einsum(
        "hqk,qhd->khd", grad_logits, queries, preferred_element_type=jnp.float32
    ) * HD ** (-0.5)
    stacked = jnp.stack([grad_queries, grad_keys, grad_values], axis=1)
    return stacked.reshape(block.shape).astype(jnp.bfloat16)


def local(
    patches,
    lengths,
    script,
    script_table,
    gain_one,
    bias_one,
    qkv_weight,
    query_bias,
    value_bias,
    out_weight,
    out_bias,
    gain_two,
    bias_two,
    up_weight,
    up_bias,
    down_weight,
    down_bias,
    cotangent,
):
    strips, row_count, model_width = patches.shape
    groups = script_table.shape[0]
    tokens = strips * row_count
    selector = (script[:, None] == jnp.arange(groups, dtype=jnp.int32)[None, :]).astype(jnp.float32)
    added = jnp.dot(selector.astype(jnp.bfloat16), script_table, preferred_element_type=jnp.float32)
    hidden = (patches.astype(jnp.float32) + added[:, None, :]).reshape(tokens, model_width)
    normed_one, inverse_one = normalize(hidden)
    inputs_one = (normed_one * gain_one + bias_one).astype(jnp.bfloat16)
    joint_bias = jnp.concatenate([query_bias, jnp.zeros_like(query_bias), value_bias])
    projected = (
        jnp.dot(inputs_one, qkv_weight, preferred_element_type=jnp.float32) + joint_bias
    ).astype(jnp.bfloat16)
    projected = projected.reshape(strips, row_count, 3, model_width)
    head_blocks = lax.all_to_all(projected, "seq", split_axis=3, concat_axis=1, tiled=True)
    mixed_heads, log_totals = lax.map(attend_forward, (head_blocks, lengths))
    mixed = lax.all_to_all(mixed_heads, "seq", split_axis=1, concat_axis=2, tiled=True).reshape(
        tokens, model_width
    )
    attended = hidden + jnp.dot(mixed, out_weight, preferred_element_type=jnp.float32) + out_bias
    normed_two, inverse_two = normalize(attended)
    inputs_two = (normed_two * gain_two + bias_two).astype(jnp.bfloat16)
    upper = jnp.dot(inputs_two, up_weight, preferred_element_type=jnp.float32) + up_bias
    active = jax.nn.gelu(upper, approximate=False).astype(jnp.bfloat16)
    result = attended + jnp.dot(active, down_weight, preferred_element_type=jnp.float32) + down_bias
    layer_out = result.astype(jnp.bfloat16).reshape(strips, row_count, model_width)
    grad_result = cotangent.reshape(tokens, model_width)
    grad_float = grad_result.astype(jnp.float32)
    grad_down_weight = weight_grad(active, grad_result)
    grad_down_bias = jnp.sum(grad_float, axis=0)
    grad_upper = (input_grad(grad_result, down_weight) * gelu_slope(upper)).astype(jnp.bfloat16)
    grad_up_weight = weight_grad(inputs_two, grad_upper)
    grad_up_bias = jnp.sum(grad_upper.astype(jnp.float32), axis=0)
    grad_inputs_two = input_grad(grad_upper, up_weight)
    grad_gain_two = jnp.sum(grad_inputs_two * normed_two, axis=0)
    grad_bias_two = jnp.sum(grad_inputs_two, axis=0)
    grad_attended = grad_float + norm_back(grad_inputs_two, gain_two, normed_two, inverse_two)
    grad_branch = grad_attended.astype(jnp.bfloat16)
    grad_out_weight = weight_grad(mixed, grad_branch)
    grad_out_bias = jnp.sum(grad_branch.astype(jnp.float32), axis=0)
    grad_mixed = (
        input_grad(grad_branch, out_weight)
        .astype(jnp.bfloat16)
        .reshape(strips, row_count, model_width)
    )
    grad_mixed_heads = lax.all_to_all(grad_mixed, "seq", split_axis=2, concat_axis=1, tiled=True)
    grad_heads = lax.map(attend_backward, (head_blocks, log_totals, grad_mixed_heads, lengths))
    grad_projected = lax.all_to_all(
        grad_heads, "seq", split_axis=1, concat_axis=3, tiled=True
    ).reshape(tokens, 3 * model_width)
    grad_qkv = weight_grad(inputs_one, grad_projected)
    grad_bias_rows = jnp.sum(grad_projected.astype(jnp.float32), axis=0)
    grad_query_bias = grad_bias_rows[:model_width]
    grad_value_bias = grad_bias_rows[2 * model_width :]
    grad_inputs_one = input_grad(grad_projected, qkv_weight)
    grad_gain_one = jnp.sum(grad_inputs_one * normed_one, axis=0)
    grad_bias_one = jnp.sum(grad_inputs_one, axis=0)
    grad_hidden = grad_attended + norm_back(grad_inputs_one, gain_one, normed_one, inverse_one)
    grad_patches = grad_hidden.astype(jnp.bfloat16).reshape(strips, row_count, model_width)
    per_strip = jnp.sum(grad_hidden.reshape(strips, row_count, model_width), axis=1)
    grad_table = jnp.dot(per_strip.T, selector, precision=lax.Precision.HIGHEST)
    summed = (
        lax.psum_scatter(grad_table, ("strip", "seq"), scatter_dimension=0, tiled=True),
        lax.psum_scatter(grad_gain_one, ("strip", "seq"), scatter_dimension=0, tiled=True),
        lax.psum_scatter(grad_bias_one, ("strip", "seq"), scatter_dimension=0, tiled=True),
        lax.psum_scatter(grad_qkv, ("strip", "seq"), scatter_dimension=0, tiled=True),
        lax.psum_scatter(grad_query_bias, ("strip", "seq"), scatter_dimension=0, tiled=True),
        lax.psum_scatter(grad_value_bias, ("strip", "seq"), scatter_dimension=0, tiled=True),
        lax.psum_scatter(grad_out_weight, ("strip", "seq"), scatter_dimension=0, tiled=True),
        lax.psum_scatter(grad_out_bias, ("strip", "seq"), scatter_dimension=0, tiled=True),
        lax.psum_scatter(grad_gain_two, ("strip", "seq"), scatter_dimension=0, tiled=True),
        lax.psum_scatter(grad_bias_two, ("strip", "seq"), scatter_dimension=0, tiled=True),
        lax.psum_scatter(grad_up_weight, ("strip", "seq"), scatter_dimension=0, tiled=True),
        lax.psum_scatter(grad_up_bias, ("strip", "seq"), scatter_dimension=0, tiled=True),
        lax.psum_scatter(grad_down_weight, ("strip", "seq"), scatter_dimension=0, tiled=True),
        lax.psum_scatter(grad_down_bias, ("strip", "seq"), scatter_dimension=0, tiled=True),
    )
    return (
        layer_out,
        grad_patches,
        summed[0],
        summed[1],
        summed[2],
        summed[3],
        summed[4],
        summed[5],
        summed[6],
        summed[7],
        summed[8],
        summed[9],
        summed[10],
        summed[11],
        summed[12],
        summed[13],
    )


def solution(mesh):
    placed = (
        P("strip", "seq", None),
        P("strip"),
        P("strip"),
        P(),
        P(),
        P(),
        P(),
        P(),
        P(),
        P(),
        P(),
        P(),
        P(),
        P(),
        P(),
        P(),
        P(),
        P("strip", "seq", None),
    )
    return jax.shard_map(
        local,
        mesh=mesh,
        in_specs=placed,
        out_specs=(
            P("strip", "seq", None),
            P("strip", "seq", None),
            P(("strip", "seq"), None),
            P(("strip", "seq")),
            P(("strip", "seq")),
            P(("strip", "seq"), None),
            P(("strip", "seq")),
            P(("strip", "seq")),
            P(("strip", "seq"), None),
            P(("strip", "seq")),
            P(("strip", "seq")),
            P(("strip", "seq")),
            P(("strip", "seq"), None),
            P(("strip", "seq")),
            P(("strip", "seq"), None),
            P(("strip", "seq")),
        ),
        check_vma=False,
    )
```

profile of v0, /device:TPU:0, one launch (start us, length us, event | category | flops | bytes accessed | tf_op | source)
XLA Modules:
  0.0 786.1 jit_solution(12835965384405361480)
XLA Ops:
  10.6 2.6 multiply_reduce_fusion.6
  17.2 3.0 add_convert_fusion.1
  21.7 2.8 reshape.248
  25.4 5.2 add_convert_fusion
  30.5 7.7 reshape.249
  38.3 10.1 %copy.125 = bf16[4,134,3,768]{1,0,2,3:T(4,128)(2,1)} copy(bf16[4,134,3,768]{3,2,1,0:T(4,128)(2,1)} %reshape.249) | data formatting | bytes 4939776 | tf_op jit(solution)/shard_map/reshape | solution.py:125
  48.4 5.1 all-to-all-start
  53.5 54.5 %all-to-all-done = bf16[4,134,3,768]{1,0,2,3:T(4,128)(2,1)} async-done(((bf16[4,134,3,768]{1,0,2,3:T(4,128)(2,1)}), bf16[4,134,3,768]{1,0,2,3:T(4,128)(2,1)}, u32[]{:S(2)}, u32[]{:S(2)}) %all-to-all-start) | async-done | bytes 2469920 | tf_op jit(solution)/shard_map/all_to_all | solution.py:126
  108.0 8.1 %copy.158 = bf16[4,4,134,3,192]{2,1,4,3,0:T(4,128)(2,1)} copy(bf16[4,4,134,3,192]{2,0,3,4,1:T(4,128)(2,1)} %bitcast.23) | data formatting | bytes 4939776 | tf_op jit(solution)/shard_map/while | solution.py:127
  116.2 8.7 %reshape.260 = bf16[4,536,3,192]{1,3,2,0:T(8,128)(2,1)} reshape(bf16[4,4,134,3,192]{2,1,4,3,0:T(4,128)(2,1)} %copy.158) | data formatting | bytes 4939776 | tf_op jit(solution)/shard_map/while | solution.py:127
  124.9 27.9 %while.22 = (s32[]{:T(128)}, bf16[4,536,192]{1,2,0:T(8,128)(2,1)}, f32[4,3,536]{2,1,0:T(4,128)}, bf16[4,536,3,192]{1,3,2,0:T(8,128)(2,1)}, s32[4]{0:T(128)S(1)}, /*index=5*/s32[]{:T(128)}) while((s32[]{:T(128)}, bf16[4,536,192]{1,2,0:T(8,128)(2,1)}, f32[4,3,536]{2,1,0:T(4,128)}, bf16[4,536,3,192]{1,3,2,0:T(8,128)(2,1)}, s32[4]{0:T(128)S(1)}, ...), condition=%wide.region_5.6_spmd, body=%wide.region_2.5_spmd.sunk | while | flops 231087808 | bytes 14145945 | solution.py:127
  152.8 3.3 copy.129
  156.0 4.5 all-to-all-start.1
  162.7 2.3 reshape.252
  164.9 10.6 %all-to-all-done.1 = bf16[4,536,192]{2,0,1:T(4,128)(2,1)} async-done(((bf16[4,536,192]{2,0,1:T(4,128)(2,1)}), bf16[4,536,192]{2,0,1:T(4,128)(2,1)}, u32[]{:S(2)}, u32[]{:S(2)}) %all-to-all-start.1) | async-done | bytes 823328 | tf_op jit(solution)/shard_map/all_to_all | solution.py:128
  178.3 3.1 reshape.250
  181.4 3.1 fusion.51
  184.9 20.2 %fusion.19 = (bf16[536,3072]{1,0:T(8,128)(2,1)}, f32[536,3072]{1,0:T(8,128)S(1)}) fusion(f32[3072]{0:T(1024)S(1)} %copy-done.19, bf16[768,3072]{1,0:T(8,128)(2,1)} %param.35, f32[536,768]{1,0:T(8,128)S(1)} %get-tuple-element.262, f32[768]{0:T(1024)S(1)} %copy-done.9, f32[768]{0:T(1024)S(1)} %copy-done.8, f32[536]{0:T(1024)S(1)} %add_rsqrt_fusion.1, ...), kind=kOutput, calls=%fused_computation.36 | convolution fusion | flops 2639898624 | bytes 16267456 | tf_op jit(solution)/shard_map/dot_general | solution.py:134
  205.2 5.9 convert_reduce_fusion.1
  211.0 3.7 multiply_reduce_fusion.1
  221.2 3.5 copy.133
  224.7 4.4 all-to-all-start.2
  229.2 4.2 fusion.42
  233.4 15.8 %all-to-all-done.2 = bf16[4,134,768]{1,0,2:T(4,128)(2,1)} async-done(((bf16[4,134,768]{1,0,2:T(4,128)(2,1)}), bf16[4,134,768]{1,0,2:T(4,128)(2,1)}, u32[]{:S(2)}, u32[]{:S(2)}) %all-to-all-start.2) | async-done | bytes 823328 | tf_op jit(solution)/shard_map/all_to_all | solution.py:157
  249.2 3.9 copy.154
  253.1 4.1 reshape.257
  257.1 45.3 %while.23 = (s32[]{:T(128)}, bf16[4,536,3,192]{1,3,2,0:T(8,128)(2,1)}, bf16[4,536,3,192]{1,3,2,0:T(8,128)(2,1)}, s32[4]{0:T(128)}, f32[4,3,536]{2,1,0:T(4,128)}, /*index=5*/bf16[4,536,192]{1,2,0:T(8,128)(2,1)}, s32[]{:T(128)}) while((s32[]{:T(128)}, bf16[4,536,3,192]{1,3,2,0:T(8,128)(2,1)}, bf16[4,536,3,192]{1,3,2,0:T(8,128)(2,1)}, ...), condition=%wide.region_12.13_spmd, body=%wide.region_10.12_spmd.sunk | while | flops 566902528 | bytes 32199044 | solution.py:158
  302.4 7.7 copy.138
  310.0 4.7 all-to-all-start.3
  319.2 34.6 %all-to-all-done.3 = bf16[4,536,3,192]{3,0,2,1:T(4,128)(2,1)} async-done(((bf16[4,536,3,192]{3,0,2,1:T(4,128)(2,1)}), bf16[4,536,3,192]{3,0,2,1:T(4,128)(2,1)}, u32[]{:S(2)}, u32[]{:S(2)}) %all-to-all-start.3) | async-done | bytes 2469920 | tf_op jit(solution)/shard_map/all_to_all | solution.py:159
  353.8 2.4 copy.167
  356.3 3.0 copy.140
  359.2 6.8 reshape.254
  366.0 7.8 fusion.53
  373.9 10.2 %fusion.45 = f32[768,3072]{1,0:T(8,128)} fusion(bf16[536,3072]{1,0:T(8,128)(2,1)} %copy-done.6, f32[536,768]{1,0:T(8,128)} %copy-done.3, f32[768]{0:T(1024)S(1)} %copy-done.9, f32[768]{0:T(1024)S(1)} %copy-done.8, f32[536]{0:T(1024)S(1)} %add_rsqrt_fusion.1, f32[536]{0:T(1024)S(1)} %broadcast_multiply_fusion.5), kind=kOutput, calls=%fused_computation.107 | convolution fusion | flops 2531223552 | bytes 14387392 | tf_op jit(solution)/shard_map/dot_general | solution.py:26
  384.4 9.9 %fusion.54 = f32[3072,768]{1,0:T(8,128)} fusion(bf16[536,3072]{1,0:T(8,128)(2,1)} %get-tuple-element.263, bf16[536,768]{1,0:T(8,128)(2,1)} %reshape.252), kind=kOutput, calls=%fused_computation.116 | convolution fusion | flops 2529165312 | bytes 13553664 | tf_op jit(solution)/shard_map/dot_general | solution.py:26
  395.9 7.7 add_convert_fusion.2
  403.6 2.3 reshape.251
  405.9 2.4 copy.143
  408.3 5.5 multiply_reduce_fusion.2
  415.9 2.8 reshape.256
  420.9 2.4 convert_reduce_fusion
  426.3 44.2 %all-reduce.10 = (f32[768,4]{0,1:T(4,128)}, f32[768]{0:T(1024)}, f32[768]{0:T(1024)}, f32[768]{0:T(1024)}, f32[768]{0:T(1024)}, /*index=5*/f32[768]{0:T(1024)}, ...) all-reduce(f32[768,4]{0,1:T(4,128)} %fusion.38, ...), channel_id=2, replica_groups=mesh['strip'=8,'seq'=4] {'strip','seq'}, use_global_device_ids=true, to_apply=%region_16.17.clone | all-reduce | flops 12288 | bytes 98304
  480.6 2.3 reshape.255
  482.9 2.4 copy.144
  487.8 8.3 %reduce-scatter.6.cloned.1.call-done = f32[24,2304]{1,0:T(8,128)} async-done(((f32[768,2304]{1,0:T(8,128)}), f32[24,2304]{1,0:T(8,128)}) %reduce-scatter.6.cloned.1.call-update) | async-done | bytes 221200 | tf_op jit(solution)/shard_map/reduce_scatter | solution.py:177
  496.1 141.7 %reduce-scatter.10.cloned.1.call-done = f32[24,3072]{1,0:T(8,128)} async-done(((f32[768,3072]{1,0:T(8,128)}), f32[24,3072]{1,0:T(8,128)}) %reduce-scatter.10.cloned.1.call-update) | async-done | bytes 294928 | tf_op jit(solution)/shard_map/reduce_scatter | solution.py:184
  637.8 141.5 %reduce-scatter.12.cloned.1.call-done = f32[96,768]{1,0:T(8,128)} async-done(((f32[3072,768]{1,0:T(8,128)}), f32[96,768]{1,0:T(8,128)}) %reduce-scatter.12.cloned.1.call-update) | async-done | bytes 294928 | tf_op jit(solution)/shard_map/reduce_scatter | solution.py:186
  (204 shorter events, 120.8 us)
Async XLA Ops:
  7.2 18.2 %copy-start = (bf16[768,2304]{1,0:T(8,128)(2,1)S(1)}, bf16[768,2304]{1,0:T(8,128)(2,1)}, u32[]{:S(2)}) copy-start(bf16[768,2304]{1,0:T(8,128)(2,1)} %param.28) | copy-start | bytes 10616836
  9.9 0.6 copy-start.7
  20.2 4.3 copy-start.17
  20.2 5.2 copy-start.10
  24.6 6.0 copy-start.13
  24.6 5.9 copy-start.15
  48.4 59.6 %all-to-all-start = ((bf16[4,134,3,768]{1,0,2,3:T(4,128)(2,1)}), bf16[4,134,3,768]{1,0,2,3:T(4,128)(2,1)}, u32[]{:S(2)}, u32[]{:S(2)}) async-start(bf16[4,134,3,768]{1,0,2,3:T(4,128)(2,1)} %copy.125), calls=%async_computation | async-start | bytes 9437184 | tf_op jit(solution)/shard_map/all_to_all | solution.py:126
  116.1 8.7 %copy-start.21 = (s32[4]{0:T(128)S(1)}, s32[4]{0:T(128)}, u32[]{:S(2)}) copy-start(s32[4]{0:T(128)} %param.23) | copy-start | bytes 52
  156.0 19.5 %all-to-all-start.1 = ((bf16[4,536,192]{2,0,1:T(4,128)(2,1)}), bf16[4,536,192]{2,0,1:T(4,128)(2,1)}, u32[]{:S(2)}, u32[]{:S(2)}) async-start(bf16[4,536,192]{2,0,1:T(4,128)(2,1)} %copy.129), calls=%async_computation.1 | async-start | bytes 2195456 | tf_op jit(solution)/shard_map/all_to_all | solution.py:128
  164.9 16.4 %copy-start.20 = (f32[768]{0:T(1024)S(1)}, f32[768]{0:T(1024)}, u32[]{:S(2)}) copy-start(f32[768]{0:T(1024)} %param.32) | copy-start | bytes 9220
  181.3 3.5 copy-start.8
  181.3 3.5 copy-start.9
  181.3 3.5 copy-start.19
  181.4 23.8 %slice-start.2 = ((s8[4718592]{0:T(1024)(128)(4,1)}), s8[4194304]{0:T(1024)(128)(4,1)S(1)}, s32[]{:S(2)}) async-start(s8[4718592]{0:T(1024)(128)(4,1)} %bitcast.162), calls=%async_computation.14 | async-start | bytes 8388608
  181.4 29.7 %slice-start = ((s8[4718592]{0:T(1024)(128)(4,1)}), s8[4194304]{0:T(1024)(128)(4,1)S(1)}, s32[]{:S(2)}) async-start(s8[4718592]{0:T(1024)(128)(4,1)} %bitcast.160), calls=%async_computation.12 | async-start | bytes 8388608
  184.5 30.2 %copy-start.3 = (f32[536,768]{1,0:T(8,128)}, f32[536,768]{1,0:T(8,128)S(1)}, u32[]{:S(2)}) copy-start(f32[536,768]{1,0:T(8,128)S(1)} %get-tuple-element.262) | copy-start | bytes 4939780
  184.9 20.2 %copy-start.5 = (bf16[536,768]{1,0:T(8,128)(2,1)S(1)}, bf16[536,768]{1,0:T(8,128)(2,1)}, u32[]{:S(2)}) copy-start(bf16[536,768]{1,0:T(8,128)(2,1)} %reshape.252) | copy-start | bytes 2469892
  184.9 20.2 %slice-start.3 = ((s8[4718592]{0:T(1024)(128)(4,1)}), s8[524288]{0:T(1024)(128)(4,1)S(1)}, s32[]{:S(2)}) async-start(s8[4718592]{0:T(1024)(128)(4,1)} %bitcast.162), calls=%async_computation.15 | async-start | bytes 1048576
  184.9 26.1 %slice-start.1 = ((s8[4718592]{0:T(1024)(128)(4,1)}), s8[524288]{0:T(1024)(128)(4,1)S(1)}, s32[]{:S(2)}) async-start(s8[4718592]{0:T(1024)(128)(4,1)} %bitcast.160), calls=%async_computation.13 | async-start | bytes 1048576
  211.0 3.7 copy-start.6
  214.7 2.5 copy-start.18
  216.0 1.2 copy-start.1
  224.7 24.5 %all-to-all-start.2 = ((bf16[4,134,768]{1,0,2:T(4,128)(2,1)}), bf16[4,134,768]{1,0,2:T(4,128)(2,1)}, u32[]{:S(2)}, u32[]{:S(2)}) async-start(bf16[4,134,768]{1,0,2:T(4,128)(2,1)} %copy.133), calls=%async_computation.2 | async-start | bytes 3145728 | tf_op jit(solution)/shard_map/all_to_all | solution.py:157
  229.1 258.7 %reduce-scatter.8.cloned.1.call-start = ((), (), s32[]{:S(2)}) async-start(), calls=%async_computation.9 | async-start | bytes 2433024 | tf_op jit(solution)/shard_map/reduce_scatter | solution.py:180
  258.3 1.6 copy-start.22
  269.6 1.6 copy-start.22
  280.9 1.6 copy-start.22
  292.2 1.6 copy-start.22
  310.0 43.8 %all-to-all-start.3 = ((bf16[4,536,3,192]{3,0,2,1:T(4,128)(2,1)}), bf16[4,536,3,192]{3,0,2,1:T(4,128)(2,1)}, u32[]{:S(2)}, u32[]{:S(2)}) async-start(bf16[4,536,3,192]{3,0,2,1:T(4,128)(2,1)} %copy.138), calls=%async_computation.3 | async-start | bytes 6586368 | tf_op jit(solution)/shard_map/all_to_all | solution.py:159
  314.8 181.3 %reduce-scatter.6.cloned.1.call-start = ((), (), s32[]{:S(2)}) async-start(), calls=%async_computation.8 | async-start | bytes 7299072 | tf_op jit(solution)/shard_map/reduce_scatter | solution.py:177
  373.9 263.9 %reduce-scatter.10.cloned.1.call-start = ((), (), s32[]{:S(2)}) async-start(), calls=%async_computation.10 | async-start | bytes 9732096 | tf_op jit(solution)/shard_map/reduce_scatter | solution.py:184
  384.1 395.2 %reduce-scatter.12.cloned.1.call-start = ((), (), s32[]{:S(2)}) async-start(), calls=%async_computation.11 | async-start | bytes 9732096 | tf_op jit(solution)/shard_map/reduce_scatter | solution.py:186
  395.9 12.5 %copy-start.11 = (f32[768]{0:T(1024)S(1)}, f32[768]{0:T(1024)}, u32[]{:S(2)}) copy-start(f32[768]{0:T(1024)} %param.26) | copy-start | bytes 9220
  395.9 12.5 %copy-start.14 = (f32[536]{0:T(1024)S(1)}, f32[536]{0:T(1024)}, u32[]{:S(2)}) copy-start(f32[536]{0:T(1024)} %copy-done.13) | copy-start | bytes 6436
  395.9 12.4 %copy-start.16 = (f32[536]{0:T(1024)S(1)}, f32[536]{0:T(1024)}, u32[]{:S(2)}) copy-start(f32[536]{0:T(1024)} %copy-done.15) | copy-start | bytes 6436
  408.3 5.6 copy-start.2
  408.3 5.6 copy-start.4
  418.8 7.6 copy-start.12
Sparse Core Ops, SparseCore 0:
  235.8 102.1 reduce-scatter.7
  374.0 122.0 reduce-scatter.5
  502.6 135.1 reduce-scatter.9
  644.1 135.1 reduce-scatter.11
where the time goes:
time: 795 us; the launch traced here: 786 us
  waiting for transfers between devices  407 us (51%)
  local copies, waits for them, and re-layouts  146 us (18%)
  matrix products  116 us (15%)
  blocking collectives  44.2 us (6%)
  other arithmetic  39.8 us (5%)
  starting transfers between devices  19 us (2%)
  between operations  14.3 us (2%)
    reduce_scatter x1, waiting for transfers between devices, local(): lax.psum_scatter(grad_up_weight, ('strip', 'seq'), scatter_dimension=0, t...  142 us
    reduce_scatter x1, waiting for transfers between devices, local(): lax.psum_scatter(grad_down_weight, ('strip', 'seq'), scatter_dimension=0,...  141 us
    all_to_all x1, waiting for transfers between devices, local(): lax.all_to_all(projected, 'seq', split_axis=3, concat_axis=1, tiled=True)  54.5 us
    unnamed x1, blocking collectives  44.2 us
    all_to_all x1, waiting for transfers between devices, local(): lax.all_to_all(grad_heads, 'seq', split_axis=1, concat_axis=3, tiled=True)  34.6 us
    dot_general x4, matrix products, weight_grad(): lax.dot_general(inputs, upstream, (((0,), (0,)), ((), ())), preferred_ele...  32.1 us
    unnamed x67, local copies, waits for them, and re-layouts  24 us
    dot_general x1, matrix products, local(): jnp.dot(inputs_two, up_weight, preferred_element_type=jnp.float32) + up_bias  20.2 us
  transfers between devices with their start and end apart: 8, of which 7 were waited for; matrix products, arithmetic and copies ran while one was open for 21% of the time, Pallas kernels for 0%

commit v1 on v0

--- a/solution.py
+++ b/solution.py
@@ -154,7 +154,10 @@
         .astype(jnp.bfloat16)
         .reshape(strips, row_count, model_width)
     )
-    grad_mixed_heads = lax.all_to_all(grad_mixed, "seq", split_axis=2, concat_axis=1, tiled=True)
+    grad_mixed_heads = jnp.concatenate(
+        lax.all_to_all(jnp.stack(jnp.split(grad_mixed, lax.axis_size("seq"), axis=2)), "seq", 0, 0),
+        axis=1,
+    )
     grad_heads = lax.map(attend_backward, (head_blocks, log_totals, grad_mixed_heads, lengths))
     grad_projected = lax.all_to_all(
         grad_heads, "seq", split_axis=1, concat_axis=3, tiled=True

time: 795 us -> 786 us (0.989)
    unnamed x67 -> x69, local copies, waits for them, and re-layouts: 24 us -> 24 us
  transfers between devices with their start and end apart: 8 -> 8, of which waited for: 7 -> 7; matrix products, arithmetic and copies ran while one was open for 21% -> 20% of each run, Pallas kernels for 0% -> 0%
where the time goes in v1:
time: 786 us; the launch traced here: 777 us
  waiting for transfers between devices  404 us (51%)
  local copies, waits for them, and re-layouts  141 us (18%)
  matrix products  115 us (15%)
  blocking collectives  43.3 us (6%)
  other arithmetic  40.1 us (5%)
  starting transfers between devices  18.9 us (2%)
  between operations  14.3 us (2%)
    reduce_scatter x1, waiting for transfers between devices, local(): lax.psum_scatter(grad_up_weight, ('strip', 'seq'), scatter_dimension=0, t...  142 us
    reduce_scatter x1, waiting for transfers between devices, local(): lax.psum_scatter(grad_down_weight, ('strip', 'seq'), scatter_dimension=0,...  141 us
    all_to_all x1, waiting for transfers between devices, local(): lax.all_to_all(projected, 'seq', split_axis=3, concat_axis=1, tiled=True)  54.5 us
    unnamed x1, blocking collectives  43.3 us
    all_to_all x1, waiting for transfers between devices, local(): lax.all_to_all(grad_heads, 'seq', split_axis=1, concat_axis=3, tiled=True)  36.6 us
    dot_general x4, matrix products, weight_grad(): lax.dot_general(inputs, upstream, (((0,), (0,)), ((), ())), preferred_ele...  32.1 us
    unnamed x69, local copies, waits for them, and re-layouts  24 us
    dot_general x1, matrix products, local(): jnp.dot(inputs_two, up_weight, preferred_element_type=jnp.float32) + up_bias  20.2 us
  transfers between devices with their start and end apart: 8, of which 7 were waited for; matrix products, arithmetic and copies ran while one was open for 20% of the time, Pallas kernels for 0%

profile of v1, /device:TPU:0, one launch (start us, length us, event | category | flops | bytes accessed | tf_op | source)
XLA Modules:
  0.0 777.2 jit_solution(4830970862818303687)
XLA Ops:
  10.6 2.6 multiply_reduce_fusion.6
  17.2 3.0 add_convert_fusion.1
  21.7 2.8 reshape.254
  25.4 5.2 add_convert_fusion
  30.5 7.7 reshape.255
  38.3 10.1 %copy.123 = bf16[4,134,3,768]{1,0,2,3:T(4,128)(2,1)} copy(bf16[4,134,3,768]{3,2,1,0:T(4,128)(2,1)} %reshape.255) | data formatting | bytes 4939776 | tf_op jit(solution)/shard_map/reshape | solution.py:125
  48.4 5.1 all-to-all-start
  53.5 54.5 %all-to-all-done = bf16[4,134,3,768]{1,0,2,3:T(4,128)(2,1)} async-done(((bf16[4,134,3,768]{1,0,2,3:T(4,128)(2,1)}), bf16[4,134,3,768]{1,0,2,3:T(4,128)(2,1)}, u32[]{:S(2)}, u32[]{:S(2)}) %all-to-all-start) | async-done | bytes 2469920 | tf_op jit(solution)/shard_map/all_to_all | solution.py:126
  108.0 8.1 %copy.154 = bf16[4,4,134,3,192]{2,1,4,3,0:T(4,128)(2,1)} copy(bf16[4,4,134,3,192]{2,0,3,4,1:T(4,128)(2,1)} %bitcast.23) | data formatting | bytes 4939776 | tf_op jit(solution)/shard_map/while | solution.py:127
  116.2 8.7 %reshape.267 = bf16[4,536,3,192]{1,3,2,0:T(8,128)(2,1)} reshape(bf16[4,4,134,3,192]{2,1,4,3,0:T(4,128)(2,1)} %copy.154) | data formatting | bytes 4939776 | tf_op jit(solution)/shard_map/while | solution.py:127
  124.9 27.9 %while.22 = (s32[]{:T(128)}, bf16[4,536,192]{1,2,0:T(8,128)(2,1)}, f32[4,3,536]{2,1,0:T(4,128)}, bf16[4,536,3,192]{1,3,2,0:T(8,128)(2,1)}, s32[4]{0:T(128)S(1)}, /*index=5*/s32[]{:T(128)}) while((s32[]{:T(128)}, bf16[4,536,192]{1,2,0:T(8,128)(2,1)}, f32[4,3,536]{2,1,0:T(4,128)}, bf16[4,536,3,192]{1,3,2,0:T(8,128)(2,1)}, s32[4]{0:T(128)S(1)}, ...), condition=%wide.region_5.6_spmd, body=%wide.region_2.5_spmd.sunk | while | flops 231087808 | bytes 14145945 | solution.py:127
  152.8 3.3 copy.127
  156.0 4.5 all-to-all-start.1
  162.7 2.3 reshape.258
  164.9 10.6 %all-to-all-done.1 = bf16[4,536,192]{2,0,1:T(4,128)(2,1)} async-done(((bf16[4,536,192]{2,0,1:T(4,128)(2,1)}), bf16[4,536,192]{2,0,1:T(4,128)(2,1)}, u32[]{:S(2)}, u32[]{:S(2)}) %all-to-all-start.1) | async-done | bytes 823328 | tf_op jit(solution)/shard_map/all_to_all | solution.py:128
  178.3 3.1 reshape.256
  181.4 3.1 fusion.51
  184.9 20.2 %fusion.19 = (bf16[536,3072]{1,0:T(8,128)(2,1)}, f32[536,3072]{1,0:T(8,128)S(1)}) fusion(f32[3072]{0:T(1024)S(1)} %copy-done.19, bf16[768,3072]{1,0:T(8,128)(2,1)} %param.35, f32[536,768]{1,0:T(8,128)S(1)} %get-tuple-element.266, f32[768]{0:T(1024)S(1)} %copy-done.9, f32[768]{0:T(1024)S(1)} %copy-done.8, f32[536]{0:T(1024)S(1)} %add_rsqrt_fusion.1, ...), kind=kOutput, calls=%fused_computation.36 | convolution fusion | flops 2639898624 | bytes 16267456 | tf_op jit(solution)/shard_map/dot_general | solution.py:134
  205.2 5.7 convert_reduce_fusion.1
  210.9 3.7 multiply_reduce_fusion.1
  218.8 2.3 reshape.259
  224.3 4.3 all-to-all-start.2
  228.6 4.2 fusion.42
  232.9 10.7 %all-to-all-done.2 = bf16[4,4,134,192]{3,1,2,0:T(4,128)(2,1)} async-done(((bf16[4,4,134,192]{3,1,2,0:T(4,128)(2,1)}), bf16[4,4,134,192]{3,1,2,0:T(4,128)(2,1)}, u32[]{:S(2)}, u32[]{:S(2)}) %all-to-all-start.2) | async-done | bytes 823328 | tf_op jit(solution)/shard_map/all_to_all | solution.py:158
  243.6 3.6 copy.134
  247.2 45.4 %while.23 = (s32[]{:T(128)}, bf16[4,536,3,192]{1,3,2,0:T(8,128)(2,1)}, bf16[4,536,3,192]{1,3,2,0:T(8,128)(2,1)}, s32[4]{0:T(128)}, f32[4,3,536]{2,1,0:T(4,128)}, /*index=5*/bf16[4,536,192]{1,2,0:T(8,128)(2,1)}, s32[]{:T(128)}) while((s32[]{:T(128)}, bf16[4,536,3,192]{1,3,2,0:T(8,128)(2,1)}, bf16[4,536,3,192]{1,3,2,0:T(8,128)(2,1)}, ...), condition=%wide.region_12.13_spmd, body=%wide.region_10.12_spmd.sunk | while | flops 566902528 | bytes 32199044 | solution.py:161
  292.6 7.7 copy.135
  300.3 4.7 all-to-all-start.3
  307.2 2.3 convert_element_type.94
  309.5 36.6 %all-to-all-done.3 = bf16[4,536,3,192]{3,0,2,1:T(4,128)(2,1)} async-done(((bf16[4,536,3,192]{3,0,2,1:T(4,128)(2,1)}), bf16[4,536,3,192]{3,0,2,1:T(4,128)(2,1)}, u32[]{:S(2)}, u32[]{:S(2)}) %all-to-all-start.3) | async-done | bytes 2469920 | tf_op jit(solution)/shard_map/all_to_all | solution.py:162
  346.1 2.4 copy.162
  348.5 3.0 copy.137
  351.4 6.8 reshape.262
  358.2 7.8 %fusion.53 = f32[768,2304]{1,0:T(8,128)} fusion(bf16[536,768]{1,0:T(8,128)(2,1)} %convert_element_type.94, bf16[536,2304]{1,0:T(8,128)(2,1)} %reshape.262), kind=kOutput, calls=%fused_computation.120 | convolution fusion | flops 1896873984 | bytes 10371072 | tf_op jit(solution)/shard_map/dot_general | solution.py:26
  366.1 10.2 %fusion.45 = f32[768,3072]{1,0:T(8,128)} fusion(bf16[536,3072]{1,0:T(8,128)(2,1)} %copy-done.6, f32[536,768]{1,0:T(8,128)} %copy-done.3, f32[768]{0:T(1024)S(1)} %copy-done.9, f32[768]{0:T(1024)S(1)} %copy-done.8, f32[536]{0:T(1024)S(1)} %add_rsqrt_fusion.1, f32[536]{0:T(1024)S(1)} %broadcast_multiply_fusion.5), kind=kOutput, calls=%fused_computation.112 | convolution fusion | flops 2531223552 | bytes 14387392 | tf_op jit(solution)/shard_map/dot_general | solution.py:26
  376.6 9.9 %fusion.54 = f32[3072,768]{1,0:T(8,128)} fusion(bf16[536,3072]{1,0:T(8,128)(2,1)} %get-tuple-element.267, bf16[536,768]{1,0:T(8,128)(2,1)} %reshape.258), kind=kOutput, calls=%fused_computation.121 | convolution fusion | flops 2529165312 | bytes 13553664 | tf_op jit(solution)/shard_map/dot_general | solution.py:26
  388.0 7.8 add_convert_fusion.2
  395.8 2.3 reshape.257
  398.1 2.4 copy.140
  400.5 5.5 multiply_reduce_fusion.2
  408.1 2.8 reshape.264
  413.1 2.4 convert_reduce_fusion
  418.5 43.3 %all-reduce.10 = (f32[768,4]{0,1:T(4,128)}, f32[768]{0:T(1024)}, f32[768]{0:T(1024)}, f32[768]{0:T(1024)}, f32[768]{0:T(1024)}, /*index=5*/f32[768]{0:T(1024)}, ...) all-reduce(f32[768,4]{0,1:T(4,128)} %fusion.38, ...), channel_id=2, replica_groups=mesh['strip'=8,'seq'=4] {'strip','seq'}, use_global_device_ids=true, to_apply=%region_16.17.clone | all-reduce | flops 12288 | bytes 98304
  471.9 2.3 reshape.263
  474.2 2.4 copy.141
  479.2 8.1 %reduce-scatter.6.cloned.1.call-done = f32[24,2304]{1,0:T(8,128)} async-done(((f32[768,2304]{1,0:T(8,128)}), f32[24,2304]{1,0:T(8,128)}) %reduce-scatter.6.cloned.1.call-update) | async-done | bytes 221200 | tf_op jit(solution)/shard_map/reduce_scatter | solution.py:180
  487.2 141.7 %reduce-scatter.10.cloned.1.call-done = f32[24,3072]{1,0:T(8,128)} async-done(((f32[768,3072]{1,0:T(8,128)}), f32[24,3072]{1,0:T(8,128)}) %reduce-scatter.10.cloned.1.call-update) | async-done | bytes 294928 | tf_op jit(solution)/shard_map/reduce_scatter | solution.py:187
  628.9 141.5 %reduce-scatter.12.cloned.1.call-done = f32[96,768]{1,0:T(8,128)} async-done(((f32[3072,768]{1,0:T(8,128)}), f32[96,768]{1,0:T(8,128)}) %reduce-scatter.12.cloned.1.call-update) | async-done | bytes 294928 | tf_op jit(solution)/shard_map/reduce_scatter | solution.py:189
  (207 shorter events, 119.6 us)
Async XLA Ops:
  7.2 18.2 %copy-start = (bf16[768,2304]{1,0:T(8,128)(2,1)S(1)}, bf16[768,2304]{1,0:T(8,128)(2,1)}, u32[]{:S(2)}) copy-start(bf16[768,2304]{1,0:T(8,128)(2,1)} %param.28) | copy-start | bytes 10616836
  9.9 0.6 copy-start.7
  20.2 4.3 copy-start.17
  20.2 5.2 copy-start.10
  24.6 6.0 copy-start.13
  24.6 5.9 copy-start.15
  48.4 59.6 %all-to-all-start = ((bf16[4,134,3,768]{1,0,2,3:T(4,128)(2,1)}), bf16[4,134,3,768]{1,0,2,3:T(4,128)(2,1)}, u32[]{:S(2)}, u32[]{:S(2)}) async-start(bf16[4,134,3,768]{1,0,2,3:T(4,128)(2,1)} %copy.123), calls=%async_computation | async-start | bytes 9437184 | tf_op jit(solution)/shard_map/all_to_all | solution.py:126
  116.1 8.7 %copy-start.22 = (s32[4]{0:T(128)S(1)}, s32[4]{0:T(128)}, u32[]{:S(2)}) copy-start(s32[4]{0:T(128)} %param.23) | copy-start | bytes 52
  156.0 19.5 %all-to-all-start.1 = ((bf16[4,536,192]{2,0,1:T(4,128)(2,1)}), bf16[4,536,192]{2,0,1:T(4,128)(2,1)}, u32[]{:S(2)}, u32[]{:S(2)}) async-start(bf16[4,536,192]{2,0,1:T(4,128)(2,1)} %copy.127), calls=%async_computation.1 | async-start | bytes 2195456 | tf_op jit(solution)/shard_map/all_to_all | solution.py:128
  164.9 16.4 %copy-start.20 = (f32[768]{0:T(1024)S(1)}, f32[768]{0:T(1024)}, u32[]{:S(2)}) copy-start(f32[768]{0:T(1024)} %param.32) | copy-start | bytes 9220
  181.3 3.5 copy-start.8
  181.3 3.5 copy-start.9
  181.3 3.5 copy-start.19
  181.4 23.8 %slice-start.2 = ((s8[4718592]{0:T(1024)(128)(4,1)}), s8[4194304]{0:T(1024)(128)(4,1)S(1)}, s32[]{:S(2)}) async-start(s8[4718592]{0:T(1024)(128)(4,1)} %bitcast.167), calls=%async_computation.14 | async-start | bytes 8388608
  181.4 29.5 %slice-start = ((s8[4718592]{0:T(1024)(128)(4,1)}), s8[4194304]{0:T(1024)(128)(4,1)S(1)}, s32[]{:S(2)}) async-start(s8[4718592]{0:T(1024)(128)(4,1)} %bitcast.165), calls=%async_computation.12 | async-start | bytes 8388608
  184.5 30.1 %copy-start.3 = (f32[536,768]{1,0:T(8,128)}, f32[536,768]{1,0:T(8,128)S(1)}, u32[]{:S(2)}) copy-start(f32[536,768]{1,0:T(8,128)S(1)} %get-tuple-element.266) | copy-start | bytes 4939780
  184.9 20.2 %copy-start.5 = (bf16[536,768]{1,0:T(8,128)(2,1)S(1)}, bf16[536,768]{1,0:T(8,128)(2,1)}, u32[]{:S(2)}) copy-start(bf16[536,768]{1,0:T(8,128)(2,1)} %reshape.258) | copy-start | bytes 2469892
  184.9 20.2 %slice-start.3 = ((s8[4718592]{0:T(1024)(128)(4,1)}), s8[524288]{0:T(1024)(128)(4,1)S(1)}, s32[]{:S(2)}) async-start(s8[4718592]{0:T(1024)(128)(4,1)} %bitcast.167), calls=%async_computation.15 | async-start | bytes 1048576
  184.9 26.0 %slice-start.1 = ((s8[4718592]{0:T(1024)(128)(4,1)}), s8[524288]{0:T(1024)(128)(4,1)S(1)}, s32[]{:S(2)}) async-start(s8[4718592]{0:T(1024)(128)(4,1)} %bitcast.165), calls=%async_computation.13 | async-start | bytes 1048576
  210.9 3.7 copy-start.6
  214.6 2.5 copy-start.18
  215.9 1.2 copy-start.1
  224.3 19.3 %all-to-all-start.2 = ((bf16[4,4,134,192]{3,1,2,0:T(4,128)(2,1)}), bf16[4,4,134,192]{3,1,2,0:T(4,128)(2,1)}, u32[]{:S(2)}, u32[]{:S(2)}) async-start(bf16[4,4,134,192]{3,1,2,0:T(4,128)(2,1)} %copy.131), calls=%async_computation.2 | async-start | bytes 2195456 | tf_op jit(solution)/shard_map/all_to_all | solution.py:158
  228.6 250.6 %reduce-scatter.8.cloned.1.call-start = ((), (), s32[]{:S(2)}) async-start(), calls=%async_computation.9 | async-start | bytes 2433024 | tf_op jit(solution)/shard_map/reduce_scatter | solution.py:183
  248.4 1.6 copy-start.23
  259.7 1.6 copy-start.23
  271.0 1.6 copy-start.23
  282.4 1.6 copy-start.23
  300.3 45.8 %all-to-all-start.3 = ((bf16[4,536,3,192]{3,0,2,1:T(4,128)(2,1)}), bf16[4,536,3,192]{3,0,2,1:T(4,128)(2,1)}, u32[]{:S(2)}, u32[]{:S(2)}) async-start(bf16[4,536,3,192]{3,0,2,1:T(4,128)(2,1)} %copy.135), calls=%async_computation.3 | async-start | bytes 6586368 | tf_op jit(solution)/shard_map/all_to_all | solution.py:162
  305.0 182.3 %reduce-scatter.6.cloned.1.call-start = ((), (), s32[]{:S(2)}) async-start(), calls=%async_computation.8 | async-start | bytes 7299072 | tf_op jit(solution)/shard_map/reduce_scatter | solution.py:180
  366.1 262.8 %reduce-scatter.10.cloned.1.call-start = ((), (), s32[]{:S(2)}) async-start(), calls=%async_computation.10 | async-start | bytes 9732096 | tf_op jit(solution)/shard_map/reduce_scatter | solution.py:187
  376.3 394.1 %reduce-scatter.12.cloned.1.call-start = ((), (), s32[]{:S(2)}) async-start(), calls=%async_computation.11 | async-start | bytes 9732096 | tf_op jit(solution)/shard_map/reduce_scatter | solution.py:189
  386.4 1.6 copy-start.21
  395.8 4.7 copy-start.11
  395.8 4.7 copy-start.14
  395.8 4.7 copy-start.16
  400.5 5.6 copy-start.2
  400.5 5.5 copy-start.4
  410.9 7.6 copy-start.12
Sparse Core Ops, SparseCore 0:
  235.3 102.7 reduce-scatter.7
  366.2 120.9 reduce-scatter.5
  493.7 135.1 reduce-scatter.9
  635.2 135.1 reduce-scatter.11
